TPU v7x, 512 devices: a whole 4x4x16 slice. The times are simulated.
512 devices in a mesh: box: 16 (over x, y_hi, core), sib: 2 (over y_lo), grp: 16 (over z).
Axes of the slice: x: 4, y: 4 (y_hi: 2, y_lo: 2; y = y_hi * 2 + y_lo), z: 16, core: 2. Of those that a mesh axis runs over, the one named last changes fastest.
Arguments:
- interface_maps: float32 [2, 32, 1024, 1024], P('sib', 'box', 'grp'), parts along dimension 1, may hold values from -1 to 1
- pivot_inverses: float32 [2, 32, 512, 512], P('sib', 'box', None, 'grp'), parts along dimension 1, may hold values from -1 to 5
- exterior_coupling: float32 [32, 1024, 5120], P('box', 'sib', 'grp'), parts along dimension 0, may hold values from -1 to 1
- face_blocks: int32 [32, 8], P('box'), parts along dimension 0, may hold values from 0 to 7, each once within a row
Outputs:
- interface_schur: float32 [32, 1024, 1024], P('box', 'sib', 'grp'), parts along dimension 0
- exterior_update: float32 [32, 1024, 5120], P('box', 'sib', 'grp'), parts along dimension 0
- multipliers: float32 [32, 1024, 1024], P('box', 'grp', 'sib'), parts along dimension 0
There are 16 independent parts, one for each index of `box`. A program takes and returns all parts, laid end to end along the dimension named above; each array names one. Nothing has to cross between parts.
Inputs may be any that keep to these rules, and one draw needn't show every extreme that they name: `face_blocks`: each row is an ordering of the 8 blocks of one child: row 0 for the first child, row 1 for the second.
All inputs are finite; a program needn't handle non-finite values.
Results may differ from a plain program's by a relative error of at most 0.0001.
Values sent between devices are 32-bit elements; how exact they have to be, the bound alone decides.
A program may use at most 128 MiB of HBM per device.

v0:
```python
import jax
import jax.numpy as jnp
from jax import lax
from jax.sharding import PartitionSpec as P


def partner(block, axis, bit):
    count = lax.axis_size(axis)
    route = []
    for low in range(count):
        high = low | 1 << bit
        if high != low and high < count:
            route += [(low, high), (high, low)]
    return lax.ppermute(block, axis, route)


def in_blocks(shard, dim, count):
    dims = shard.shape
    pieces = shard.reshape(*dims[:dim], count, dims[dim] // count, *dims[dim + 1 :])
    return jnp.moveaxis(pieces, dim, 0)


def summed_on_arrival(shard, axis, dim):
    pieces = in_blocks(shard, dim, lax.axis_size(axis))
    arrived = lax.all_to_all(pieces, axis, split_axis=0, concat_axis=0, tiled=True)
    return arrived.sum(axis=0)


def in_one_piece(arrays, axis, dim, along):
    ends, at = ([], 0)
    for a in arrays[:-1]:
        at += a.shape[along]
        ends.append(at)
    both = jnp.concatenate(arrays, axis=along)
    return tuple(jnp.split(summed_on_arrival(both, axis, dim), ends, axis=along))


def complex_dot(left_side, right_side):

    def product(first_part, second_part):
        return jnp.dot(
            first_part,
            second_part,
            precision=lax.Precision.HIGHEST,
            preferred_element_type=jnp.float32,
        )

    real_part = product(left_side[0], right_side[0]) - product(left_side[1], right_side[1])
    imag_part = product(left_side[0], right_side[1]) + product(left_side[1], right_side[0])
    return jnp.stack([real_part, imag_part])


def block_sources(face_blocks):
    alpha_order = face_blocks[0]
    beta_order = face_blocks[1]
    slots = jnp.arange(face_blocks.shape[1], dtype=jnp.int32)
    beta_match = (beta_order[:, None] == slots[None, :]).astype(jnp.int32)
    alpha_match = (alpha_order[:, None] == slots[None, :]).astype(jnp.int32)
    to_beta = jnp.sum(beta_match * alpha_order[:, None], axis=0)
    to_alpha = jnp.sum(alpha_match * beta_order[:, None], axis=0)
    return (to_beta, to_alpha)


def reorder(matrix, source):
    blocks = source.shape[0]
    grouped = matrix.reshape(matrix.shape[0], blocks, matrix.shape[1] // blocks, matrix.shape[2])
    return jnp.take(grouped, source, axis=1).reshape(matrix.shape)


def per_device(interface_maps, pivot_inverses, exterior_coupling, face_blocks):
    own_rows = interface_maps[0]
    partner_rows = partner(own_rows, "sib", 0)
    sibling = lax.axis_index("sib")
    member = lax.axis_index("grp")
    alpha_rows = jnp.where(sibling == 0, own_rows, partner_rows)
    beta_rows = jnp.where(sibling == 0, partner_rows, own_rows)
    local_rows = own_rows.shape[1]
    order_size = own_rows.shape[2]
    panel_width = pivot_inverses.shape[2]
    half_rows = order_size // 2
    to_beta, to_alpha = block_sources(face_blocks)
    panel_section = lax.dynamic_slice_in_dim(alpha_rows, sibling * panel_width, panel_width, 2)
    raw_multipliers = complex_dot(
        panel_section, lax.all_gather(pivot_inverses, "grp", axis=3, tiled=True)[0]
    )
    beta_cols = lax.all_to_all(beta_rows, "grp", split_axis=2, concat_axis=1, tiled=True)
    beta_perm = reorder(beta_cols, to_alpha)
    local_cols = beta_perm.shape[2]
    beta_panel = lax.dynamic_slice_in_dim(beta_perm, sibling * panel_width, panel_width, 1)
    piece = lax.all_gather(raw_multipliers, "grp", axis=1, tiled=True)
    joined = jnp.concatenate(
        [piece, -complex_dot(piece, beta_panel), complex_dot(piece, exterior_coupling)], axis=2
    )
    joined = reorder(joined, to_beta)
    multipliers = lax.dynamic_slice_in_dim(
        joined[:, :, :panel_width], member * local_rows, local_rows, 1
    )
    partial_schur = joined[:, :, panel_width : panel_width + local_cols]
    partial_exterior = joined[:, :, panel_width + local_cols :]
    summed_schur, exterior_update = in_one_piece((partial_schur, partial_exterior), "sib", 1, 2)
    row_index = sibling * half_rows + jnp.arange(half_rows, dtype=jnp.int32)
    col_index = member * local_cols + jnp.arange(local_cols, dtype=jnp.int32)
    identity_real = (row_index[:, None] == col_index[None, :]).astype(jnp.float32)
    identity_block = jnp.stack([identity_real, jnp.zeros_like(identity_real)])
    interface_schur = identity_block + summed_schur
    return (interface_schur, exterior_update, multipliers)


def solution(mesh):
    in_specs = (
        P("sib", "box", "grp", None),
        P("sib", "box", None, "grp"),
        P("box", "sib", "grp"),
        P("box", None),
    )
    out_specs = (P("box", "sib", "grp"), P("box", "sib", "grp"), P("box", "grp", "sib"))
    return jax.shard_map(
        per_device, mesh=mesh, in_specs=in_specs, out_specs=out_specs, check_vma=False
    )
```

profile of v0, /device:TPU:4, one launch (start us, length us, event | category | flops | bytes accessed | tf_op | source)
XLA Modules:
  0.0 277.3 jit_solution(12519139690456995614)
XLA Ops:
  7.2 0.0 all-gather.3.cloned.1.call-start
  7.2 0.7 all-gather.3.cloned.1.call-update
  7.9 0.0 all-gather.5.cloned.1.call-start
  7.9 3.5 %collective-permute-start = (f32[2,64,1024]{2,1,0:T(8,128)}, f32[2,64,1024]{2,1,0:T(8,128)S(1)}, u32[]{:S(2)}, u32[]{:S(2)}) collective-permute-start(f32[2,64,1024]{2,1,0:T(8,128)} %bitcast.121), channel_id=1, source_target_pairs={{0,16},{16,0},{1,17},{17,1},{2,18},{18,2},{3,19},{19,3},{4,20},{20... | collective-permute-start | bytes 1572872 | tf_op jit(solution)/shard_map/ppermute | solution.py:14
  11.4 12.3 %collective-permute-done = f32[2,64,1024]{2,1,0:T(8,128)S(1)} collective-permute-done((f32[2,64,1024]{2,1,0:T(8,128)}, f32[2,64,1024]{2,1,0:T(8,128)S(1)}, u32[]{:S(2)}, u32[]{:S(2)}) %collective-permute-start) | collective-permute-done | bytes 524320 | tf_op jit(solution)/shard_map/ppermute | solution.py:14
  23.7 1.0 dynamic-slice_select_fusion.1
  24.7 62.4 %all-gather.3.cloned.1.call-done = f32[1,2,512,512]{2,3,1,0:T(8,128)} async-done(((f32[1,2,512,32]{2,3,1,0:T(8,128)}), f32[1,2,512,512]{2,3,1,0:T(8,128)}) %all-gather.3.cloned.1.call-update) | async-done | bytes 2097168 | tf_op jit(solution)/shard_map/all_gather | solution.py:84
  87.1 2.5 fusion.19
  89.6 2.3 fusion.18
  91.9 0.0 copy-done.3
  91.9 0.0 copy-start.5
  91.9 1.1 fusion.17
  93.0 1.1 fusion.16
  94.2 0.7 pad_maximum_fusion.2
  94.9 0.0 all-gather.5.cloned.1.call-update
  94.9 0.0 copy-done.5
  94.9 0.1 broadcast_select_fusion
  95.0 0.0 copy-start.6
  95.0 0.6 copy.106
  95.6 1.9 reshape.137
  97.5 8.0 %all-to-all-start = ((f32[16,1,8192]{2,1,0:T(1,128)}), f32[16,1,8192]{2,1,0:T(1,128)S(1)}, u32[]{:S(2)}, u32[]{:S(2)}) async-start(f32[16,1,8192]{2,1,0:T(1,128)} %reshape.137), calls=%async_computation | async-start | bytes 1048576 | tf_op jit(solution)/shard_map/all_to_all | solution.py:86
  105.5 0.0 copy-done.6
  105.5 0.1 select_reduce_fusion.1
  105.6 0.1 broadcast_bitcast_fusion
  105.7 0.1 dynamic-slice
  105.8 0.1 broadcast_bitcast_fusion.1
  105.9 24.2 %all-to-all-done = f32[16,1,8192]{2,1,0:T(1,128)S(1)} async-done(((f32[16,1,8192]{2,1,0:T(1,128)}), f32[16,1,8192]{2,1,0:T(1,128)S(1)}, u32[]{:S(2)}, u32[]{:S(2)}) %all-to-all-start) | async-done | bytes 524320 | tf_op jit(solution)/shard_map/all_to_all | solution.py:86
  130.0 0.5 broadcast.132
  130.6 1.9 reduce
  132.5 0.8 reshape.138
  133.2 0.6 copy.123
  133.8 0.2 reshape.118
  134.0 0.1 copy.108
  134.2 0.6 gather_fusion
  134.8 43.9 %all-gather.5.cloned.1.call-done = f32[2,1024,512]{2,1,0:T(8,128)} async-done(((f32[2,64,512]{2,1,0:T(8,128)}), f32[2,1024,512]{2,1,0:T(8,128)}) %all-gather.5.cloned.1.call-update) | async-done | bytes 4194320 | tf_op jit(solution)/shard_map/all_gather | solution.py:90
  178.7 3.9 %fusion.3 = f32[1024,64]{0,1:T(8,128)S(1)} fusion(f32[2,1024,512]{2,1,0:T(8,128)} %all-gather.5.cloned.1.call-done, f32[2,512,64]{1,2,0:T(8,128)S(1)} %dynamic-slice_select_fusion), kind=kOutput, calls=%fused_computation.10 | convolution fusion | flops 402653184 | bytes 2490368 | tf_op jit(solution)/shard_map/dot_general | solution.py:41
  182.6 3.7 %fusion.2 = f32[1024,64]{0,1:T(8,128)S(1)} fusion(f32[2,1024,512]{2,1,0:T(8,128)} %all-gather.5.cloned.1.call-done, f32[2,512,64]{1,2,0:T(8,128)S(1)} %dynamic-slice_select_fusion), kind=kOutput, calls=%fused_computation.9 | convolution fusion | flops 402653184 | bytes 2490368 | tf_op jit(solution)/shard_map/dot_general | solution.py:41
  186.3 2.2 fusion.13
  188.5 2.2 fusion.15
  190.7 1.3 copy.110
  192.0 4.3 %fusion.1 = f32[1024,320]{0,1:T(8,128)S(1)} fusion(f32[2,1024,512]{2,1,0:T(8,128)} %all-gather.5.cloned.1.call-done, f32[2,512,320]{1,2,0:T(8,128)S(1)} %copy-done.4), kind=kOutput, calls=%fused_computation.8 | convolution fusion | flops 2013265920 | bytes 4063232 | tf_op jit(solution)/shard_map/dot_general | solution.py:41
  196.3 3.9 %fusion = f32[1024,320]{0,1:T(8,128)S(1)} fusion(f32[2,1024,512]{2,1,0:T(8,128)} %all-gather.5.cloned.1.call-done, f32[2,512,320]{1,2,0:T(8,128)S(1)} %copy-done.4), kind=kOutput, calls=%fused_computation.7 | convolution fusion | flops 2013265920 | bytes 4063232 | tf_op jit(solution)/shard_map/dot_general | solution.py:41
  200.3 2.4 fusion.9
  202.7 2.4 fusion.11
  205.1 1.7 pad_maximum_fusion.1
  206.8 2.3 copy.111
  209.1 5.5 %pad_maximum_fusion = f32[2,1024,896]{2,1,0:T(8,128)} fusion(f32[2,1024,320]{2,1,0:T(8,128)S(1)} %copy.111, f32[2,1024,64]{2,1,0:T(8,128)} %copy.110, f32[2,1024,512]{2,1,0:T(8,128)} %all-gather.5.cloned.1.call-done), kind=kLoop, calls=%fused_computation.2 | loop fusion | flops 3670016 | bytes 14680064 | tf_op jit(solution)/shard_map/concatenate | solution.py:91
  214.6 7.1 %gather_fusion.1 = f32[8,2,128,896]{3,2,1,0:T(8,128)} fusion(f32[2,8,128,896]{3,2,1,0:T(8,128)} %bitcast.116, s32[1024]{0:T(1024)S(1)} %pad_clamp_fusion), kind=kCustom, calls=%fused_computation.1 | custom fusion | bytes 14680096 | tf_op jit(solution)/shard_map/jit(_take)/gather | solution.py:67
  221.7 3.8 %copy.112 = f32[2,8,128,896]{3,2,1,0:T(8,128)S(1)} copy(f32[2,8,128,896]{3,2,0,1:T(8,128)} %bitcast.115) | data formatting | bytes 14680064 | tf_op jit(solution)/shard_map/jit(_take)/gather | solution.py:67
  225.5 0.6 bitcast_select_fusion
  226.0 2.9 %copy-done.2 = f32[2,1024,896]{2,1,0:T(8,128)} copy-done((f32[2,1024,896]{2,1,0:T(8,128)}, f32[2,1024,896]{2,1,0:T(8,128)S(1)}, u32[]{:S(2)}) %copy-start.2) | copy-done | bytes 7340056
  229.0 0.2 concatenate.8
  229.2 1.9 copy.113
  231.1 3.9 %all-to-all-start.1 = ((f32[2,2,512,384]{3,2,1,0:T(8,128)}), f32[2,2,512,384]{3,2,1,0:T(8,128)S(1)}, u32[]{:S(2)}, u32[]{:S(2)}) async-start(f32[2,2,512,384]{3,2,1,0:T(8,128)} %copy.113), calls=%async_computation.1 | async-start | bytes 6291456 | tf_op jit(solution)/shard_map/all_to_all | solution.py:25
  235.1 0.1 broadcast_compare_fusion
  235.2 0.0 slice-start
  235.2 2.2 slice-done
  237.4 0.7 constant_dynamic-slice_fusion
  238.1 25.5 %all-to-all-done.1 = f32[2,2,512,384]{3,2,1,0:T(8,128)S(1)} async-done(((f32[2,2,512,384]{3,2,1,0:T(8,128)}), f32[2,2,512,384]{3,2,1,0:T(8,128)S(1)}, u32[]{:S(2)}, u32[]{:S(2)}) %all-to-all-start.1) | async-done | bytes 3145760 | tf_op jit(solution)/shard_map/all_to_all | solution.py:25
  263.6 1.5 reduce_sum.35
  265.1 1.9 split.9
  267.0 1.5 copy.116
  268.5 1.1 slice_add_fusion
  269.6 0.9 copy.115
  (19 shorter events, 0.2 us)
Async XLA Ops:
  7.2 79.9 %all-gather.3.cloned.1.call-start = ((), (), s32[]{:S(2)}) async-start(), calls=%async_computation.2 | async-start | bytes 2228224 | tf_op jit(solution)/shard_map/all_gather | solution.py:84
  7.9 170.8 %all-gather.5.cloned.1.call-start = ((), (), s32[]{:S(2)}) async-start(), calls=%async_computation.3 | async-start | bytes 4456448 | tf_op jit(solution)/shard_map/all_gather | solution.py:90
  7.9 15.8 %collective-permute-start = (f32[2,64,1024]{2,1,0:T(8,128)}, f32[2,64,1024]{2,1,0:T(8,128)S(1)}, u32[]{:S(2)}, u32[]{:S(2)}) collective-permute-start(f32[2,64,1024]{2,1,0:T(8,128)} %bitcast.121), channel_id=1, source_target_pairs={{0,16},{16,0},{1,17},{17,1},{2,18},{18,2},{3,19},{19,3},{4,20},{20... | collective-permute-start | bytes 1572872 | tf_op jit(solution)/shard_map/ppermute | solution.py:14
  87.1 4.8 %copy-start.3 = (f32[1,2,512,512]{2,3,1,0:T(8,128)S(1)}, f32[1,2,512,512]{2,3,1,0:T(8,128)}, u32[]{:S(2)}) copy-start(f32[1,2,512,512]{2,3,1,0:T(8,128)} %all-gather.3.cloned.1.call-done) | copy-start | bytes 6291460
  91.9 3.0 %copy-start.5 = (f32[1,2,64,1024]{3,2,1,0:T(8,128)S(1)}, f32[1,2,64,1024]{3,2,1,0:T(8,128)}, u32[]{:S(2)}) copy-start(f32[1,2,64,1024]{3,2,1,0:T(8,128)} %param.4) | copy-start | bytes 1572868
  95.0 10.5 %copy-start.6 = (s32[2,8]{1,0:T(2,128)S(1)}, s32[2,8]{1,0:T(2,128)}, u32[]{:S(2)}) copy-start(s32[2,8]{1,0:T(2,128)} %param.7) | copy-start | bytes 196
  97.5 32.6 %all-to-all-start = ((f32[16,1,8192]{2,1,0:T(1,128)}), f32[16,1,8192]{2,1,0:T(1,128)S(1)}, u32[]{:S(2)}, u32[]{:S(2)}) async-start(f32[16,1,8192]{2,1,0:T(1,128)} %reshape.137), calls=%async_computation | async-start | bytes 1048576 | tf_op jit(solution)/shard_map/all_to_all | solution.py:86
  178.7 7.6 %copy-start = (f32[2,1024,512]{2,1,0:T(8,128)S(1)}, f32[2,1024,512]{2,1,0:T(8,128)}, u32[]{:S(2)}) copy-start(f32[2,1024,512]{2,1,0:T(8,128)} %all-gather.5.cloned.1.call-done) | copy-start | bytes 12582916
  188.5 3.5 %copy-start.4 = (f32[2,512,320]{1,2,0:T(8,128)S(1)}, f32[2,512,320]{1,2,0:T(8,128)}, u32[]{:S(2)}) copy-start(f32[2,512,320]{1,2,0:T(8,128)} %param.6) | copy-start | bytes 3932164
  192.0 8.3 %copy-start.1 = (f32[2,1024,512]{2,1,0:T(8,128)S(1)}, f32[2,1024,512]{2,1,0:T(8,128)}, u32[]{:S(2)}) copy-start(f32[2,1024,512]{2,1,0:T(8,128)} %all-gather.5.cloned.1.call-done) | copy-start | bytes 12582916
  226.0 2.9 %copy-start.2 = (f32[2,1024,896]{2,1,0:T(8,128)}, f32[2,1024,896]{2,1,0:T(8,128)S(1)}, u32[]{:S(2)}) copy-start(f32[2,1024,896]{2,1,0:T(8,128)S(1)} %bitcast_select_fusion) | copy-start | bytes 22020100
  231.1 32.5 %all-to-all-start.1 = ((f32[2,2,512,384]{3,2,1,0:T(8,128)}), f32[2,2,512,384]{3,2,1,0:T(8,128)S(1)}, u32[]{:S(2)}, u32[]{:S(2)}) async-start(f32[2,2,512,384]{3,2,1,0:T(8,128)} %copy.113), calls=%async_computation.1 | async-start | bytes 6291456 | tf_op jit(solution)/shard_map/all_to_all | solution.py:25
  235.2 2.2 slice-start
Sparse Core Ops, SparseCore 0:
  10.1 76.9 all-gather.2
  95.0 83.6 all-gather.4
where the time goes:
time: 278 us; the launch traced here: 277 us
  waiting for transfers between devices  169 us (61%)
  local copies, waits for them, and re-layouts  32.3 us (12%)
  matrix products  32 us (12%)
  starting transfers between devices  15.5 us (6%)
  between operations  14.4 us (5%)
  other arithmetic  14.3 us (5%)
    all_gather x1, waiting for transfers between devices, per_device(): lax.all_gather(pivot_inverses, 'grp', axis=3, tiled=True)[0]  62.4 us
    all_gather x1, waiting for transfers between devices, per_device(): piece = lax.all_gather(raw_multipliers, 'grp', axis=1, tiled=True)  43.9 us
    dot_general x12, matrix products, product(): jnp.dot(first_part, second_part, precision=lax.Precision.HIGHEST, preferr...  32 us
    all_to_all x1, waiting for transfers between devices, summed_on_arrival(): lax.all_to_all(pieces, axis, split_axis=0, concat_axis=0, tiled=True)  25.5 us
    all_to_all x1, waiting for transfers between devices, per_device(): lax.all_to_all(beta_rows, 'grp', split_axis=2, concat_axis=1, tiled=True)  24.2 us
    ppermute x1, waiting for transfers between devices, partner(): return lax.ppermute(block, axis, route)  12.3 us
    gather x4, local copies, waits for them, and re-layouts, reorder(): return jnp.take(grouped, source, axis=1).reshape(matrix.shape)  11.5 us
    unnamed x18, local copies, waits for them, and re-layouts  8.03 us
  transfers between devices with their start and end apart: 5, of which 5 were waited for; matrix products, arithmetic and copies ran while one was open for 3% of the time, Pallas kernels for 0%

commit v1 on v0

--- a/solution.py
+++ b/solution.py
@@ -87,7 +87,11 @@
     beta_perm = reorder(beta_cols, to_alpha)
     local_cols = beta_perm.shape[2]
     beta_panel = lax.dynamic_slice_in_dim(beta_perm, sibling * panel_width, panel_width, 1)
-    piece = lax.all_gather(raw_multipliers, "grp", axis=1, tiled=True)
+    devices = lax.axis_size("grp")
+    repeats = [devices if d == 1 else 1 for d in range(raw_multipliers.ndim)]
+    piece = lax.all_to_all(
+        jnp.tile(raw_multipliers, repeats), "grp", split_axis=1, concat_axis=1, tiled=True
+    )
     joined = jnp.concatenate(
         [piece, -complex_dot(piece, beta_panel), complex_dot(piece, exterior_coupling)], axis=2
     )

time: 278 us -> 414 us (1.49)
  the two profiles are of different devices: /device:TPU:4 before, /device:TPU:6 now
where the time goes in v1:
time: 414 us; the launch traced here: 413 us
  waiting for transfers between devices  274 us (66%)
  local copies, waits for them, and re-layouts  48.5 us (12%)
  starting transfers between devices  31 us (7%)
  matrix products  28.1 us (7%)
  other arithmetic  16.8 us (4%)
  between operations  14.4 us (3%)
    all_to_all x1, waiting for transfers between devices, per_device(): lax.all_to_all(jnp.tile(raw_multipliers, repeats), 'grp', split_axis=1, c...  169 us
    all_gather x1, waiting for transfers between devices, per_device(): lax.all_gather(pivot_inverses, 'grp', axis=3, tiled=True)[0]  59.8 us
    all_to_all x1, waiting for transfers between devices, summed_on_arrival(): lax.all_to_all(pieces, axis, split_axis=0, concat_axis=0, tiled=True)  32.4 us
    dot_general x12, matrix products, product(): jnp.dot(first_part, second_part, precision=lax.Precision.HIGHEST, preferr...  28.1 us
    all_to_all x1, starting transfers between devices, per_device(): lax.all_to_all(beta_rows, 'grp', split_axis=2, concat_axis=1, tiled=True)  15.2 us
    ppermute x1, waiting for transfers between devices, partner(): return lax.ppermute(block, axis, route)  12.3 us
    gather x4, local copies, waits for them, and re-layouts, reorder(): return jnp.take(grouped, source, axis=1).reshape(matrix.shape)  11.5 us
    all_to_all x1, starting transfers between devices, per_device(): lax.all_to_all(jnp.tile(raw_multipliers, repeats), 'grp', split_axis=1, c...  8.3 us
  transfers between devices with their start and end apart: 5, of which 4 were waited for; matrix products, arithmetic and copies ran while one was open for 4% of the time, Pallas kernels for 0%

profile of v1, /device:TPU:6, one launch (start us, length us, event | category | flops | bytes accessed | tf_op | source)
XLA Modules:
  0.0 413.2 jit_solution(12869813080577825644)
XLA Ops:
  7.2 0.0 all-gather.2.cloned.1.call-start
  7.2 0.7 all-gather.2.cloned.1.call-update
  7.9 3.5 collective-permute-start
  11.4 12.3 %collective-permute-done = f32[2,64,1024]{2,1,0:T(8,128)S(1)} collective-permute-done((f32[2,64,1024]{2,1,0:T(8,128)}, f32[2,64,1024]{2,1,0:T(8,128)S(1)}, u32[]{:S(2)}, u32[]{:S(2)}) %collective-permute-start) | collective-permute-done | bytes 524320 | tf_op jit(solution)/shard_map/ppermute | solution.py:14
  23.7 1.1 broadcast_select_fusion
  24.8 0.0 copy-start.6
  24.8 0.6 copy.46
  25.3 1.9 reshape.141
  27.2 15.2 %all-to-all-start.1 = ((f32[16,1,8192]{2,1,0:T(1,128)}), f32[16,1,8192]{2,1,0:T(1,128)S(1)}, u32[]{:S(2)}, u32[]{:S(2)}) async-start(f32[16,1,8192]{2,1,0:T(1,128)} %reshape.141), calls=%async_computation.1 | async-start | bytes 1048576 | tf_op jit(solution)/shard_map/all_to_all | solution.py:86
  42.5 59.8 %all-gather.2.cloned.1.call-done = f32[1,2,512,512]{2,3,1,0:T(8,128)} async-done(((f32[1,2,512,32]{2,3,1,0:T(8,128)}), f32[1,2,512,512]{2,3,1,0:T(8,128)}) %all-gather.2.cloned.1.call-update) | async-done | bytes 2097168 | tf_op jit(solution)/shard_map/all_gather | solution.py:84
  102.3 2.5 fusion.51
  104.8 2.3 fusion.49
  107.1 1.1 fusion.50
  108.2 1.1 fusion.48
  109.4 0.2 copy.45
  109.6 0.0 all-to-all-done.1
  109.6 3.6 tile.4
  113.2 8.3 %all-to-all-start = ((f32[2,1024,512]{2,0,1:T(2,128)}), f32[2,1024,512]{2,0,1:T(2,128)}, u32[]{:S(2)}, u32[]{:S(2)}) async-start(f32[2,1024,512]{2,0,1:T(2,128)} %bitcast.125), calls=%async_computation | async-start | bytes 8388608 | tf_op jit(solution)/shard_map/all_to_all | solution.py:92
  121.5 0.1 select_reduce_fusion.1
  121.6 0.1 broadcast_bitcast_fusion
  121.7 0.1 dynamic-slice
  121.8 0.1 broadcast_bitcast_fusion.1
  121.9 0.5 broadcast.135
  122.4 1.9 reduce
  124.3 0.8 reshape.142
  125.0 0.6 copy.116
  125.7 0.2 reshape.122
  125.9 0.1 copy.48
  126.0 0.6 gather_fusion
  126.7 0.0 copy-start.4
  126.7 169.4 %all-to-all-done = f32[2,1024,512]{2,0,1:T(2,128)} async-done(((f32[2,1024,512]{2,0,1:T(2,128)}), f32[2,1024,512]{2,0,1:T(2,128)}, u32[]{:S(2)}, u32[]{:S(2)}) %all-to-all-start) | async-done | bytes 4194336 | tf_op jit(solution)/shard_map/all_to_all | solution.py:92
  296.1 7.1 %fusion.62 = (f32[1,1024,512]{2,0,1:T(1,128)S(1)}, f32[1,1024,512]{2,0,1:T(1,128)S(1)}) fusion(f32[2,1024,512]{2,0,1:T(2,128)} %all-to-all-done), kind=kLoop, calls=%fused_computation.88 | loop fusion | bytes 8388608 | tf_op jit(solution)/shard_map/slice | solution.py:48
  303.1 0.0 copy-start.2
  303.1 2.2 fusion.6
  305.3 2.2 fusion.4
  307.5 3.7 fusion.2
  311.1 2.4 fusion
  313.5 2.2 fusion.39
  315.7 2.2 fusion.45
  317.8 0.8 maximum_negate_fusion
  318.7 2.2 copy.50
  320.8 4.0 fusion.27
  324.8 2.4 fusion.33
  327.3 1.7 pad_maximum_fusion.1
  329.0 4.5 %copy.51 = f32[2,1024,320]{2,0,1:T(2,128)S(1)} copy(f32[2,1024,320]{1,2,0:T(8,128)} %pad_maximum_fusion.1) | data formatting | bytes 5242880 | tf_op jit(solution)/shard_map/stack | solution.py:50
  333.5 7.7 %pad_maximum_fusion = f32[2,1024,896]{2,0,1:T(2,128)S(1)} fusion(f32[2,1024,320]{2,0,1:T(2,128)S(1)} %copy.51, f32[2,1024,64]{2,0,1:T(2,128)} %copy.50, f32[2,1024,512]{2,0,1:T(2,128)} %all-to-all-done), kind=kLoop, calls=%fused_computation.2 | loop fusion | flops 3670016 | bytes 14680064 | tf_op jit(solution)/shard_map/concatenate | solution.py:95
  341.2 3.4 copy.52
  344.6 7.1 %gather_fusion.1 = f32[8,2,128,896]{3,2,1,0:T(8,128)} fusion(f32[2,8,128,896]{3,2,1,0:T(8,128)} %bitcast.123, s32[1024]{0:T(1024)S(1)} %pad_clamp_fusion), kind=kCustom, calls=%fused_computation.1 | custom fusion | bytes 14680096 | tf_op jit(solution)/shard_map/jit(_take)/gather | solution.py:67
  351.7 3.8 copy.53
  355.5 0.6 bitcast_select_fusion
  356.1 0.2 concatenate.8
  356.3 2.2 copy.115
  358.5 1.6 copy-done
  360.1 3.9 all-to-all-start.2
  364.1 0.1 broadcast_compare_fusion
  364.2 0.0 slice-start
  364.2 2.2 slice-done
  366.4 0.7 constant_dynamic-slice_fusion
  367.1 32.4 %all-to-all-done.2 = f32[2,2,512,384]{3,2,1,0:T(8,128)S(1)} async-done(((f32[2,2,512,384]{3,2,1,0:T(8,128)}), f32[2,2,512,384]{3,2,1,0:T(8,128)S(1)}, u32[]{:S(2)}, u32[]{:S(2)}) %all-to-all-start.2) | async-done | bytes 3145760 | tf_op jit(solution)/shard_map/all_to_all | solution.py:25
  399.5 1.5 reduce_sum.35
  401.0 1.9 split.9
  402.9 1.5 copy.57
  404.4 1.1 slice_add_fusion
  405.5 0.9 copy.56
  (24 shorter events, 0.2 us)
Async XLA Ops:
  7.2 95.1 %all-gather.2.cloned.1.call-start = ((), (), s32[]{:S(2)}) async-start(), calls=%async_computation.3 | async-start | bytes 2228224 | tf_op jit(solution)/shard_map/all_gather | solution.py:84
  7.9 15.8 %collective-permute-start = (f32[2,64,1024]{2,1,0:T(8,128)}, f32[2,64,1024]{2,1,0:T(8,128)S(1)}, u32[]{:S(2)}, u32[]{:S(2)}) collective-permute-start(f32[2,64,1024]{2,1,0:T(8,128)} %bitcast.131), channel_id=1, source_target_pairs={{0,16},{16,0},{1,17},{17,1},{2,18},{18,2},{3,19},{19,3},{4,20},{20... | collective-permute-start | bytes 1572872 | tf_op jit(solution)/shard_map/ppermute | solution.py:14
  24.8 17.7 %copy-start.6 = (f32[1,2,64,1024]{3,2,1,0:T(8,128)S(1)}, f32[1,2,64,1024]{3,2,1,0:T(8,128)}, u32[]{:S(2)}) copy-start(f32[1,2,64,1024]{3,2,1,0:T(8,128)} %param.4) | copy-start | bytes 1572868
  27.2 82.3 %all-to-all-start.1 = ((f32[16,1,8192]{2,1,0:T(1,128)}), f32[16,1,8192]{2,1,0:T(1,128)S(1)}, u32[]{:S(2)}, u32[]{:S(2)}) async-start(f32[16,1,8192]{2,1,0:T(1,128)} %reshape.141), calls=%async_computation.1 | async-start | bytes 1048576 | tf_op jit(solution)/shard_map/all_to_all | solution.py:86
  102.3 4.8 %copy-start.1 = (f32[1,2,512,512]{2,3,1,0:T(8,128)S(1)}, f32[1,2,512,512]{2,3,1,0:T(8,128)}, u32[]{:S(2)}) copy-start(f32[1,2,512,512]{2,3,1,0:T(8,128)} %all-gather.2.cloned.1.call-done) | copy-start | bytes 6291460
  113.2 8.3 %copy-start.7 = (s32[2,8]{1,0:T(2,128)S(1)}, s32[2,8]{1,0:T(2,128)}, u32[]{:S(2)}) copy-start(s32[2,8]{1,0:T(2,128)} %param.7) | copy-start | bytes 196
  113.2 182.9 %all-to-all-start = ((f32[2,1024,512]{2,0,1:T(2,128)}), f32[2,1024,512]{2,0,1:T(2,128)}, u32[]{:S(2)}, u32[]{:S(2)}) async-start(f32[2,1024,512]{2,0,1:T(2,128)} %bitcast.125), calls=%async_computation | async-start | bytes 8388608 | tf_op jit(solution)/shard_map/all_to_all | solution.py:92
  126.7 178.6 %copy-start.4 = (f32[2,512,64]{1,2,0:T(8,128)}, f32[2,512,64]{1,2,0:T(8,128)S(1)}, u32[]{:S(2)}) copy-start(f32[2,512,64]{1,2,0:T(8,128)S(1)} %dynamic-slice_select_fusion) | copy-start | bytes 786436
  303.1 4.3 %copy-start.2 = (f32[2,512,320]{1,2,0:T(8,128)S(1)}, f32[2,512,320]{1,2,0:T(8,128)}, u32[]{:S(2)}) copy-start(f32[2,512,320]{1,2,0:T(8,128)} %param.6) | copy-start | bytes 3932164
  311.1 2.4 copy-start.5
  320.8 4.0 copy-start.3
  356.1 4.0 copy-start
  360.1 39.4 %all-to-all-start.2 = ((f32[2,2,512,384]{3,2,1,0:T(8,128)}), f32[2,2,512,384]{3,2,1,0:T(8,128)S(1)}, u32[]{:S(2)}, u32[]{:S(2)}) async-start(f32[2,2,512,384]{3,2,1,0:T(8,128)} %bitcast.126), calls=%async_computation.2 | async-start | bytes 6291456 | tf_op jit(solution)/shard_map/all_to_all | solution.py:25
  364.2 2.2 slice-start
Sparse Core Ops, SparseCore 0:
  10.1 92.1 all-gather.1
